TPU v7x, 256 devices: a whole 4x4x8 slice. The times are simulated.
256 devices in a mesh: expert: 32 (over z_hi, y, core), dp: 8 (over z_lo, x).
Axes of the slice: x: 4, y: 4, z: 8 (z_hi: 4, z_lo: 2; z = z_hi * 2 + z_lo), core: 2. Of those that a mesh axis runs over, the one named last changes fastest.
Arguments:
- tokens: bfloat16 [32768, 4096], P(('expert', 'dp')), may hold values from -6 to 6
- route: int32 [32768, 2], P(('expert', 'dp')), may hold values from 0 to 63, all different within a row; in each aligned block of 128 rows (0 to 127, 128 to 255, ...) at most 12 rows name the same one
- gate_output_gradient: bfloat16 [32768, 2, 1536], P(('expert', 'dp')), may hold values from -0.4375 to 0.4375
- frozen_gate_weight: bfloat16 [64, 4096, 1536], P('expert', 'dp'), may hold values from -0.09375 to 0.09375
- adapter_first: bfloat16 [64, 4096, 16], P('expert'), may hold values from -0.09375 to 0.09375
- adapter_second: bfloat16 [64, 16, 1536], P('expert'), may hold values from -0.15625 to 0.15625
Outputs:
- grad_a: float32 [64, 4096, 16], P('expert')
- grad_b: float32 [64, 16, 1536], P('expert')
Inputs may be any that keep to these rules, and one draw needn't show every extreme that they name: `route`: each row names 2 different experts. Within each device's aligned block of 128 rows no expert is named more than 12 times.
All inputs are finite; a program needn't handle non-finite values.
Results may differ from a plain program's by a relative error of at most 0.0043.
Values may be sent and summed in bfloat16 or wider, within the bound.
No kernel may reach another device: no remote copies, remote signals or barrier semaphores. Data moves between devices by JAX's collectives and lax.ppermute only.
A program may use at most 128 MiB of HBM per device.

v0:
```python
import jax
import jax.numpy as jnp
from jax import lax
from jax.sharding import PartitionSpec as P

ADAPTER_SCALE = 2.0


def silu_slope(gate_preactivation):
    squash = jax.nn.sigmoid(gate_preactivation)
    return squash * (1.0 + gate_preactivation * (1.0 - squash))


def block_product(input_rows, piece):
    return jnp.dot(input_rows, piece, preferred_element_type=jnp.float32)


def prepare(input_rows, rows_g):
    block = 128
    return (input_rows, rows_g, None, block)


def adapter_grads(input_rows, rows_g, frozen_output, first_adapter_factor, second_adapter_factor):
    rank_reduced_output = jnp.dot(
        input_rows, first_adapter_factor, preferred_element_type=jnp.float32
    ).astype(jnp.bfloat16)
    gate_preactivation = frozen_output + ADAPTER_SCALE * jnp.dot(
        rank_reduced_output, second_adapter_factor, preferred_element_type=jnp.float32
    )
    activation_slope = (rows_g.astype(jnp.float32) * silu_slope(gate_preactivation)).astype(
        jnp.bfloat16
    )
    up_gradient = ADAPTER_SCALE * jnp.einsum(
        "nr,nf->rf", rank_reduced_output, activation_slope, preferred_element_type=jnp.float32
    )
    rank_backward = jnp.einsum(
        "nf,rf->nr", activation_slope, second_adapter_factor, preferred_element_type=jnp.float32
    ).astype(jnp.bfloat16)
    down_gradient = ADAPTER_SCALE * jnp.einsum(
        "nd,nr->dr", input_rows, rank_backward, preferred_element_type=jnp.float32
    )
    return (down_gradient, up_gradient)


def local(tokens, route, gate_output_gradient, frozen_gate_weight, adapter_first, adapter_second):
    experts_here = frozen_gate_weight.shape[0]
    columns = lax.axis_size("expert")
    experts = experts_here * columns
    tok_rows = tokens.shape[0]
    top_count = route.shape[1]
    width = tokens.shape[1]
    hidden = gate_output_gradient.shape[2]
    capacity = 3 * tok_rows * top_count // experts
    slot_count = tok_rows * top_count
    flat_route = route.reshape(slot_count)
    labels = jnp.arange(experts, dtype=jnp.int32)
    one_hot = (flat_route[:, None] == labels[None, :]).astype(jnp.int32)
    ranks = jnp.sum((jnp.cumsum(one_hot, axis=0) - one_hot) * one_hot, axis=1)
    target = (flat_route % experts_here * columns + flat_route // experts_here) * capacity + ranks
    positions = jnp.arange(experts * capacity, dtype=jnp.int32)
    hits = target[None, :] == positions[:, None]
    filled = jnp.any(hits, axis=1)
    slot_ids = jnp.arange(slot_count, dtype=jnp.int32)
    source_slot = jnp.sum(jnp.where(hits, slot_ids[None, :], 0), axis=1)
    send_x = tokens[source_slot // top_count].reshape(experts_here, columns, capacity, width)
    flat_grad = gate_output_gradient.reshape(slot_count, hidden)
    send_g = jnp.where(
        filled[:, None], flat_grad[source_slot], jnp.zeros((), gate_output_gradient.dtype)
    )
    send_g = send_g.reshape(experts_here, columns, capacity, hidden)
    group_rows = columns * capacity
    recv_x, recv_g = (
        lax.all_to_all(send_x, "expert", split_axis=1, concat_axis=1, tiled=True),
        lax.all_to_all(send_g, "expert", split_axis=1, concat_axis=1, tiled=True),
    )
    input_rows = recv_x.reshape(experts_here, group_rows, width)
    rows_g = recv_g.reshape(experts_here, group_rows, hidden)
    ready_inputs = [
        prepare(input_rows[local_result], rows_g[local_result])
        for local_result in range(experts_here)
    ]

    def add_rows(piece):
        return jnp.stack(
            [
                block_product(ready_inputs[local_result][0], piece[local_result])
                for local_result in range(experts_here)
            ]
        )

    frozen_output = add_rows(lax.all_gather(frozen_gate_weight, "dp", axis=1, tiled=True))
    results = [
        adapter_grads(
            ready_inputs[local_result][0],
            ready_inputs[local_result][1],
            frozen_output[local_result],
            adapter_first[local_result],
            adapter_second[local_result],
        )
        for local_result in range(experts_here)
    ]
    grad_a_local = jnp.stack([result[0] for result in results])
    grad_b_local = jnp.stack([result[1] for result in results])
    grad_a, grad_b = lax.psum((grad_a_local, grad_b_local), "dp")
    return (grad_a, grad_b)


def solution(mesh):
    return jax.shard_map(
        local,
        mesh=mesh,
        in_specs=(
            P(("expert", "dp"), None),
            P(("expert", "dp"), None),
            P(("expert", "dp"), None, None),
            P("expert", "dp", None),
            P("expert", None, None),
            P("expert", None, None),
        ),
        out_specs=(P("expert", None, None), P("expert", None, None)),
        check_vma=False,
    )
```

profile of v0, /device:TPU:8, one launch (start us, length us, event | category | flops | bytes accessed | tf_op | source)
XLA Modules:
  0.0 568.3 jit_solution(11198235258273988007)
XLA Ops:
  7.2 0.7 all-gather.2.cloned.1.call-update
  9.9 3.9 gather_fusion.1
  13.7 4.8 gather.10
  18.8 2.2 broadcast_select_fusion
  21.0 3.8 copy.20
  24.8 11.7 %all-to-all-start.1 = ((bf16[2,32,12,1536]{3,0,2,1:T(2,128)(2,1)}), bf16[2,32,12,1536]{3,0,2,1:T(2,128)(2,1)S(1)}, u32[]{:S(2)}, u32[]{:S(2)}) async-start(bf16[2,32,12,1536]{3,0,2,1:T(2,128)(2,1)} %copy.20), calls=%async_computation.1 | async-start | bytes 4718592 | tf_op jit(solution)/shard_map/all_to_all | solution.py:74
  36.6 5.7 gather_fusion
  42.2 9.8 %reshape.176 = bf16[2,32,12,4096]{3,2,1,0:T(8,128)(2,1)} reshape(bf16[768,4096]{1,0:T(8,128)(2,1)} %gather_fusion) | data formatting | bytes 12582912 | tf_op jit(solution)/shard_map/reshape | solution.py:65
  52.0 13.6 %copy.19 = bf16[2,32,12,4096]{3,0,2,1:T(2,128)(2,1)} copy(bf16[2,32,12,4096]{3,2,1,0:T(8,128)(2,1)} %reshape.176) | data formatting | bytes 12582912 | tf_op jit(solution)/shard_map/reshape | solution.py:65
  65.5 53.0 %all-to-all-done.1 = bf16[2,32,12,1536]{3,0,2,1:T(2,128)(2,1)S(1)} async-done(((bf16[2,32,12,1536]{3,0,2,1:T(2,128)(2,1)}), bf16[2,32,12,1536]{3,0,2,1:T(2,128)(2,1)S(1)}, u32[]{:S(2)}, u32[]{:S(2)}) %all-to-all-start.1) | async-done | bytes 2359328 | tf_op jit(solution)/shard_map/all_to_all | solution.py:74
  118.6 5.3 all-to-all-start
  124.0 15.2 %fusion.7 = (f32[32,12,1536]{2,1,0:T(8,128)}, f32[32,12,1536]{2,1,0:T(8,128)}) fusion(bf16[2,32,12,1536]{3,0,2,1:T(2,128)(2,1)S(1)} %all-to-all-done.1), kind=kLoop, calls=%fused_computation.20 | loop fusion | flops 1179648 | bytes 7077888 | tf_op jit(solution)/shard_map/convert_element_type | solution.py:30
  139.1 3.6 reshape.178
  142.7 3.6 reshape.179
  146.2 186.4 %all-to-all-done = bf16[2,32,12,4096]{3,0,2,1:T(2,128)(2,1)} async-done(((bf16[2,32,12,4096]{3,0,2,1:T(2,128)(2,1)}), bf16[2,32,12,4096]{3,0,2,1:T(2,128)(2,1)}, u32[]{:S(2)}, u32[]{:S(2)}) %all-to-all-start) | async-done | bytes 6291488 | tf_op jit(solution)/shard_map/all_to_all | solution.py:73
  332.6 33.0 %slice_reduce_fusion.1 = (bf16[32,12,4096]{2,1,0:T(8,128)(2,1)}, bf16[32,12,4096]{2,1,0:T(8,128)(2,1)}) fusion(bf16[2,32,12,4096]{3,0,2,1:T(2,128)(2,1)} %all-to-all-done), kind=kLoop, calls=%fused_computation.7 | loop fusion | bytes 12582912 | tf_op jit(solution)/shard_map/slice | solution.py:79
  365.6 5.6 squeeze.26
  371.2 5.6 squeeze.30
  376.8 3.0 convolution_convert_fusion.3
  379.8 0.9 convolution_convert_fusion.1
  380.8 69.1 %all-gather.2.cloned.1.call-done = bf16[2,4096,1536]{2,1,0:T(8,128)(2,1)} async-done(((bf16[2,512,1536]{2,1,0:T(8,128)(2,1)}), bf16[2,4096,1536]{2,1,0:T(8,128)(2,1)}) %all-gather.2.cloned.1.call-update) | async-done | bytes 25165840 | tf_op jit(solution)/shard_map/all_gather | solution.py:91
  449.8 9.3 %fusion.1 = f32[384,1536]{1,0:T(8,128)S(1)} fusion(bf16[384,4096]{1,0:T(8,128)(2,1)} %squeeze.26, bf16[2,4096,1536]{2,1,0:T(8,128)(2,1)} %all-gather.2.cloned.1.call-done), kind=kOutput, calls=%fused_computation.5 | convolution fusion | flops 4831838208 | bytes 18087936 | tf_op jit(solution)/shard_map/dot_general | solution.py:15
  459.2 1.1 multiply_convert_fusion.1
  460.6 3.0 fusion.3
  463.6 9.1 %fusion = f32[384,1536]{1,0:T(8,128)S(1)} fusion(bf16[384,4096]{1,0:T(8,128)(2,1)} %squeeze.30, bf16[2,4096,1536]{2,1,0:T(8,128)(2,1)} %all-gather.2.cloned.1.call-done), kind=kOutput, calls=%fused_computation.3 | convolution fusion | flops 4831838208 | bytes 18087936 | tf_op jit(solution)/shard_map/dot_general | solution.py:15
  472.7 1.1 multiply_convert_fusion
  474.1 3.1 fusion.2
  477.2 0.7 pad_maximum_fusion.1
  477.9 0.8 pad_maximum_fusion
  478.7 79.3 %all-reduce.3.cloned.1.call-done = (f32[2,4096,16]{1,2,0:T(8,128)}, f32[2,16,1536]{2,1,0:T(8,128)}) async-done(((f32[2,4096,16]{1,2,0:T(8,128)}, f32[2,16,1536]{2,1,0:T(8,128)}), (f32[2,4096,16]{1,2,0:T(8,128)}, f32[2,16,1536]{2,1,0:T(8,128)})) %all-reduce.3.cloned.1.call-update) | async-done | bytes 720912 | tf_op jit(solution)/shard_map/psum | solution.py:104
  558.0 1.9 copy.29
  559.9 1.6 copy.30
  (39 shorter events, 2.9 us)
Async XLA Ops:
  7.2 29.4 %copy-start = (bf16[128,4096]{1,0:T(8,128)(2,1)S(1)}, bf16[128,4096]{1,0:T(8,128)(2,1)}, u32[]{:S(2)}) copy-start(bf16[128,4096]{1,0:T(8,128)(2,1)} %param.6) | copy-start | bytes 3145732
  7.2 0.8 copy-start.8
  7.2 2.0 copy-start.5
  7.2 442.6 %all-gather.2.cloned.1.call-start = ((), (), s32[]{:S(2)}) async-start(), calls=%async_computation.2 | async-start | bytes 28311552 | tf_op jit(solution)/shard_map/all_gather | solution.py:91
  24.8 93.7 %all-to-all-start.1 = ((bf16[2,32,12,1536]{3,0,2,1:T(2,128)(2,1)}), bf16[2,32,12,1536]{3,0,2,1:T(2,128)(2,1)S(1)}, u32[]{:S(2)}, u32[]{:S(2)}) async-start(bf16[2,32,12,1536]{3,0,2,1:T(2,128)(2,1)} %copy.20), calls=%async_computation.1 | async-start | bytes 4718592 | tf_op jit(solution)/shard_map/all_to_all | solution.py:74
  118.6 214.0 %all-to-all-start = ((bf16[2,32,12,4096]{3,0,2,1:T(2,128)(2,1)}), bf16[2,32,12,4096]{3,0,2,1:T(2,128)(2,1)}, u32[]{:S(2)}, u32[]{:S(2)}) async-start(bf16[2,32,12,4096]{3,0,2,1:T(2,128)(2,1)} %copy.19), calls=%async_computation | async-start | bytes 12582912 | tf_op jit(solution)/shard_map/all_to_all | solution.py:73
  123.9 434.1 %all-reduce.3.cloned.1.call-start = ((), (), s32[]{:S(2)}) async-start(), calls=%async_computation.3 | async-start | bytes 1441792 | tf_op jit(solution)/shard_map/psum | solution.py:104
  371.2 5.6 copy-start.6
  376.8 3.0 copy-start.2
  380.8 78.4 %copy-start.7 = (bf16[2,16,1536]{2,1,0:T(8,128)(2,1)S(1)}, bf16[2,16,1536]{2,1,0:T(8,128)(2,1)}, u32[]{:S(2)}) copy-start(bf16[2,16,1536]{2,1,0:T(8,128)(2,1)} %param.11) | copy-start | bytes 294916
  449.8 9.3 %copy-start.4 = (f32[384,1536]{1,0:T(8,128)S(1)}, f32[384,1536]{1,0:T(8,128)}, u32[]{:S(2)}) copy-start(f32[384,1536]{1,0:T(8,128)} %reshape.178) | copy-start | bytes 7077892
  463.6 9.1 %copy-start.3 = (f32[384,1536]{1,0:T(8,128)S(1)}, f32[384,1536]{1,0:T(8,128)}, u32[]{:S(2)}) copy-start(f32[384,1536]{1,0:T(8,128)} %reshape.179) | copy-start | bytes 7077892
  474.1 87.4 %copy-start.1 = (bf16[128,4096]{1,0:T(8,128)(2,1)S(1)}, bf16[128,4096]{1,0:T(8,128)(2,1)}, u32[]{:S(2)}) copy-start(bf16[128,4096]{1,0:T(8,128)(2,1)} %param.6) | copy-start | bytes 3145732
Sparse Core Ops, SparseCore 0:
  9.8 439.9 all-gather.1
  478.8 79.1 all-reduce.2
where the time goes:
time: 569 us; the launch traced here: 568 us
  waiting for transfers between devices  388 us (68%)
  local copies, waits for them, and re-layouts  97.3 us (17%)
  matrix products  31.2 us (5%)
  other arithmetic  20 us (4%)
  starting transfers between devices  17.1 us (3%)
  between operations  14.2 us (2%)
    all_to_all x1, waiting for transfers between devices, local(): lax.all_to_all(send_x, 'expert', split_axis=1, concat_axis=1, tiled=True)  186 us
    psum x1, waiting for transfers between devices, local(): grad_a, grad_b = lax.psum((grad_a_local, grad_b_local), 'dp')  79.3 us
    all_gather x1, waiting for transfers between devices, local(): lax.all_gather(frozen_gate_weight, 'dp', axis=1, tiled=True)  69.1 us
    all_to_all x1, waiting for transfers between devices, local(): lax.all_to_all(send_g, 'expert', split_axis=1, concat_axis=1, tiled=True)  53 us
    slice x1, local copies, waits for them, and re-layouts, local(): input_rows[local_result]  33 us
    reshape x2, local copies, waits for them, and re-layouts, local(): tokens[source_slot // top_count]  23.3 us
    dot_general x2, matrix products, block_product(): return jnp.dot(input_rows, piece, preferred_element_type=jnp.float32)  18.4 us
    convert_element_type x1, other arithmetic, adapter_grads(): rows_g.astype(jnp.float32) * silu_slope(gate_preactivation)  15.2 us
  transfers between devices with their start and end apart: 4, of which 4 were waited for; matrix products, arithmetic and copies ran while one was open for 20% of the time, Pallas kernels for 0%

commit v1 on v0

--- a/solution.py
+++ b/solution.py
@@ -88,7 +88,7 @@
             ]
         )
 
-    frozen_output = add_rows(lax.all_gather(frozen_gate_weight, "dp", axis=1, tiled=True))
+    frozen_output = add_rows(jnp.concatenate(lax.all_gather(frozen_gate_weight, "dp"), axis=1))
     results = [
         adapter_grads(
             ready_inputs[local_result][0],

time: 569 us -> 579 us (1.018)
  local copies, waits for them, and re-layouts: 97.3 us -> 111 us
    slice x1 -> x2, local copies, waits for them, and re-layouts: 0.18 us -> 14 us  [the longest x1 13.8 us: add_rows(): piece[local_result]]
where the time goes in v1:
time: 579 us; the launch traced here: 578 us
  waiting for transfers between devices  388 us (67%)
  local copies, waits for them, and re-layouts  111 us (19%)
  matrix products  27 us (5%)
  other arithmetic  19.9 us (3%)
  starting transfers between devices  17.3 us (3%)
  between operations  14.2 us (2%)
    all_to_all x1, waiting for transfers between devices, local(): lax.all_to_all(send_x, 'expert', split_axis=1, concat_axis=1, tiled=True)  186 us
    psum x1, waiting for transfers between devices, local(): grad_a, grad_b = lax.psum((grad_a_local, grad_b_local), 'dp')  79.3 us
    all_gather x1, waiting for transfers between devices, local(): lax.all_gather(frozen_gate_weight, 'dp')  69 us
    all_to_all x1, waiting for transfers between devices, local(): lax.all_to_all(send_g, 'expert', split_axis=1, concat_axis=1, tiled=True)  53 us
    slice x1, local copies, waits for them, and re-layouts, local(): input_rows[local_result]  33 us
    reshape x2, local copies, waits for them, and re-layouts, local(): tokens[source_slot // top_count]  23.3 us
    convert_element_type x1, other arithmetic, adapter_grads(): rows_g.astype(jnp.float32) * silu_slope(gate_preactivation)  15 us
    dot_general x2, matrix products, block_product(): return jnp.dot(input_rows, piece, preferred_element_type=jnp.float32)  14.2 us
  transfers between devices with their start and end apart: 4, of which 4 were waited for; matrix products, arithmetic and copies ran while one was open for 20% of the time, Pallas kernels for 0%

profile of v1, /device:TPU:8, one launch (start us, length us, event | category | flops | bytes accessed | tf_op | source)
XLA Modules:
  0.0 577.9 jit_solution(4415072167542892640)
XLA Ops:
  10.2 3.9 gather_fusion.1
  14.1 4.8 gather.10
  18.8 2.2 broadcast_select_fusion
  21.0 3.8 copy.20
  24.9 11.7 %all-to-all-start.1 = ((bf16[2,32,12,1536]{3,0,2,1:T(2,128)(2,1)}), bf16[2,32,12,1536]{3,0,2,1:T(2,128)(2,1)S(1)}, u32[]{:S(2)}, u32[]{:S(2)}) async-start(bf16[2,32,12,1536]{3,0,2,1:T(2,128)(2,1)} %copy.20), calls=%async_computation.1 | async-start | bytes 4718592 | tf_op jit(solution)/shard_map/all_to_all | solution.py:74
  36.6 5.7 gather_fusion
  42.2 9.8 %reshape.184 = bf16[2,32,12,4096]{3,2,1,0:T(8,128)(2,1)} reshape(bf16[768,4096]{1,0:T(8,128)(2,1)} %gather_fusion) | data formatting | bytes 12582912 | tf_op jit(solution)/shard_map/reshape | solution.py:65
  52.0 13.6 %copy.19 = bf16[2,32,12,4096]{3,0,2,1:T(2,128)(2,1)} copy(bf16[2,32,12,4096]{3,2,1,0:T(8,128)(2,1)} %reshape.184) | data formatting | bytes 12582912 | tf_op jit(solution)/shard_map/reshape | solution.py:65
  65.6 53.0 %all-to-all-done.1 = bf16[2,32,12,1536]{3,0,2,1:T(2,128)(2,1)S(1)} async-done(((bf16[2,32,12,1536]{3,0,2,1:T(2,128)(2,1)}), bf16[2,32,12,1536]{3,0,2,1:T(2,128)(2,1)S(1)}, u32[]{:S(2)}, u32[]{:S(2)}) %all-to-all-start.1) | async-done | bytes 2359328 | tf_op jit(solution)/shard_map/all_to_all | solution.py:74
  118.6 5.3 all-to-all-start
  124.1 15.0 %fusion.5 = (f32[32,12,1536]{2,1,0:T(8,128)}, f32[32,12,1536]{2,1,0:T(8,128)}) fusion(bf16[2,32,12,1536]{3,0,2,1:T(2,128)(2,1)S(1)} %all-to-all-done.1), kind=kLoop, calls=%fused_computation.16 | loop fusion | flops 1179648 | bytes 7077888 | tf_op jit(solution)/shard_map/convert_element_type | solution.py:30
  139.1 3.6 reshape.187
  142.7 3.6 reshape.188
  146.3 186.3 %all-to-all-done = bf16[2,32,12,4096]{3,0,2,1:T(2,128)(2,1)} async-done(((bf16[2,32,12,4096]{3,0,2,1:T(2,128)(2,1)}), bf16[2,32,12,4096]{3,0,2,1:T(2,128)(2,1)}, u32[]{:S(2)}, u32[]{:S(2)}) %all-to-all-start) | async-done | bytes 6291488 | tf_op jit(solution)/shard_map/all_to_all | solution.py:73
  332.6 33.0 %slice_reduce_fusion.1 = (bf16[32,12,4096]{2,1,0:T(8,128)(2,1)}, bf16[32,12,4096]{2,1,0:T(8,128)(2,1)}) fusion(bf16[2,32,12,4096]{3,0,2,1:T(2,128)(2,1)} %all-to-all-done), kind=kLoop, calls=%fused_computation.3 | loop fusion | bytes 12582912 | tf_op jit(solution)/shard_map/slice | solution.py:79
  365.6 5.7 squeeze.26
  371.2 5.6 squeeze.30
  376.9 3.0 convolution_convert_fusion.3
  379.9 0.9 convolution_convert_fusion.1
  380.8 69.0 %all-gather.3.cloned.1.call-done = bf16[16,512,1536]{2,1,0:T(8,128)(2,1)} async-done(((bf16[2,512,1536]{2,1,0:T(8,128)(2,1)}), bf16[16,512,1536]{2,1,0:T(8,128)(2,1)}) %all-gather.3.cloned.1.call-update) | async-done | bytes 25165840 | tf_op jit(solution)/shard_map/all_gather | solution.py:91
  449.8 13.8 %fusion.33 = (bf16[1,8,512,1536]{3,2,0,1:T(8,128)(2,1)S(1)}, bf16[1,8,512,1536]{3,2,0,1:T(8,128)(2,1)}) fusion(bf16[2,8,512,1536]{3,2,0,1:T(8,128)(2,1)} %bitcast.66), kind=kLoop, calls=%fused_computation.71 | loop fusion | bytes 50331648 | tf_op jit(solution)/shard_map/slice | solution.py:86
  463.6 5.1 fusion.34
  468.7 1.1 multiply_convert_fusion.1
  469.9 3.0 fusion.1
  473.1 9.1 %fusion.35 = f32[384,1536]{1,0:T(8,128)S(1)} fusion(bf16[384,4096]{1,0:T(8,128)(2,1)} %squeeze.30, bf16[4096,1536]{1,0:T(8,128)(2,1)} %bitcast.67), kind=kOutput, calls=%fused_computation.73 | convolution fusion | flops 4831838208 | bytes 18087936 | tf_op jit(solution)/shard_map/dot_general | solution.py:15
  482.2 1.1 multiply_convert_fusion
  483.4 3.1 fusion
  486.7 0.7 pad_maximum_fusion.1
  487.4 0.8 pad_maximum_fusion
  488.3 79.3 %all-reduce.3.cloned.1.call-done = (f32[2,4096,16]{1,2,0:T(8,128)}, f32[2,16,1536]{2,1,0:T(8,128)}) async-done(((f32[2,4096,16]{1,2,0:T(8,128)}, f32[2,16,1536]{2,1,0:T(8,128)}), (f32[2,4096,16]{1,2,0:T(8,128)}, f32[2,16,1536]{2,1,0:T(8,128)})) %all-reduce.3.cloned.1.call-update) | async-done | bytes 720912 | tf_op jit(solution)/shard_map/psum | solution.py:104
  567.6 1.9 copy.29
  569.4 1.6 copy.30
  (42 shorter events, 3.8 us)
Async XLA Ops:
  7.2 29.4 %copy-start = (bf16[128,4096]{1,0:T(8,128)(2,1)S(1)}, bf16[128,4096]{1,0:T(8,128)(2,1)}, u32[]{:S(2)}) copy-start(bf16[128,4096]{1,0:T(8,128)(2,1)} %param.6) | copy-start | bytes 3145732
  7.2 0.8 copy-start.9
  7.2 2.5 copy-start.6
  7.2 442.6 %all-gather.3.cloned.1.call-start = ((), (), s32[]{:S(2)}) async-start(), calls=%async_computation.2 | async-start | bytes 28311552 | tf_op jit(solution)/shard_map/all_gather | solution.py:91
  24.9 93.7 %all-to-all-start.1 = ((bf16[2,32,12,1536]{3,0,2,1:T(2,128)(2,1)}), bf16[2,32,12,1536]{3,0,2,1:T(2,128)(2,1)S(1)}, u32[]{:S(2)}, u32[]{:S(2)}) async-start(bf16[2,32,12,1536]{3,0,2,1:T(2,128)(2,1)} %copy.20), calls=%async_computation.1 | async-start | bytes 4718592 | tf_op jit(solution)/shard_map/all_to_all | solution.py:74
  118.6 214.0 %all-to-all-start = ((bf16[2,32,12,4096]{3,0,2,1:T(2,128)(2,1)}), bf16[2,32,12,4096]{3,0,2,1:T(2,128)(2,1)}, u32[]{:S(2)}, u32[]{:S(2)}) async-start(bf16[2,32,12,4096]{3,0,2,1:T(2,128)(2,1)} %copy.19), calls=%async_computation | async-start | bytes 12582912 | tf_op jit(solution)/shard_map/all_to_all | solution.py:73
  123.9 443.6 %all-reduce.3.cloned.1.call-start = ((), (), s32[]{:S(2)}) async-start(), calls=%async_computation.3 | async-start | bytes 1441792 | tf_op jit(solution)/shard_map/psum | solution.py:104
  371.2 5.6 copy-start.7
  376.9 3.0 copy-start.2
  449.8 13.8 %copy-start.3 = (bf16[384,4096]{1,0:T(8,128)(2,1)S(1)}, bf16[384,4096]{1,0:T(8,128)(2,1)}, u32[]{:S(2)}) copy-start(bf16[384,4096]{1,0:T(8,128)(2,1)} %squeeze.26) | copy-start | bytes 9437188
  463.6 5.1 copy-start.5
  463.6 5.1 copy-start.8
  473.1 9.1 %copy-start.4 = (f32[384,1536]{1,0:T(8,128)S(1)}, f32[384,1536]{1,0:T(8,128)}, u32[]{:S(2)}) copy-start(f32[384,1536]{1,0:T(8,128)} %reshape.188) | copy-start | bytes 7077892
  483.4 87.7 %copy-start.1 = (bf16[128,4096]{1,0:T(8,128)(2,1)S(1)}, bf16[128,4096]{1,0:T(8,128)(2,1)}, u32[]{:S(2)}) copy-start(bf16[128,4096]{1,0:T(8,128)(2,1)} %param.6) | copy-start | bytes 3145732
Sparse Core Ops, SparseCore 0:
  9.8 439.9 all-gather.2
  488.4 79.1 all-reduce.2
